TPU v7x, 256 devices: a whole 4x4x8 slice. The times are simulated.
256 devices in a mesh: gx: 16 (over z, core), gy: 4 (over x), gz: 4 (over y).
Axes of the slice: x: 4, y: 4, z: 8, core: 2. Of those that a mesh axis runs over, the one named last changes fastest.
Arguments:
- block_values: bfloat16 [4, 64, 4, 6, 128, 128], P('gy', 'gx', 'gz'), as said below
- block_cols: int32 [4, 64, 4, 6], P('gy', 'gx', 'gz'), may hold values from 0 to 63, as said below
Outputs:
- purified: float32 [2048, 32768], P(('gx', 'gy'), 'gz')
Inputs may be any that keep to these rules, and one draw needn't show every extreme that they name: block_cols[a, s, b, :] holds 6 distinct tile columns of panel b at which tile row a * 64 + s of P is nonzero; every tile column of a panel is listed by exactly 6 tile rows of each slab; the pattern is symmetric: tile (i, j) is listed exactly when tile (j, i) is. `block_values`: P is symmetric: the tile listed at (i, j) is the transpose of the tile listed at (j, i), and diagonal tiles are symmetric.
All inputs are finite; a program needn't handle non-finite values.
Results may differ from a plain program's by a relative error of at most 0.0033.
Values may be sent and summed in bfloat16 or wider, within the bound.
A program may use at most 128 MiB of HBM per device.

v0:
```python
import jax
import jax.numpy as jnp
from jax import lax
from jax.sharding import PartitionSpec as P

WIN = 1


def picked_2(x, axis, root):
    return lax.dynamic_index_in_dim(lax.all_gather(x, axis), root, 0, keepdims=False)


def in_blocks(x, dim, length):
    lengths = x.shape
    tiles = x.reshape(*lengths[:dim], length, lengths[dim] // length, *lengths[dim + 1 :])
    return jnp.moveaxis(tiles, dim, 0)


def sent_and_summed(x, axis, dim):
    tiles = in_blocks(x, dim, lax.axis_size(axis))
    arrived = lax.all_to_all(tiles, axis, split_axis=0, concat_axis=0, tiled=True)
    return arrived.astype(jnp.float32).sum(axis=0)


def densify(left_tiles, left_columns, slab_tiles):
    onehot = (
        left_columns[:, :, None] == jnp.arange(slab_tiles, dtype=jnp.int32)[None, None, :]
    ).astype(jnp.bfloat16)
    densified = jnp.einsum("wkj,wkyx->wyjx", onehot, left_tiles, preferred_element_type=jnp.float32)
    tile_size = left_tiles.shape[2]
    return densified.astype(jnp.bfloat16).reshape(
        left_tiles.shape[0] * tile_size, slab_tiles, tile_size
    )


def product_one(left_panel, panel_tiles, panel_columns):
    summed = jnp.zeros(
        (left_panel.shape[0], panel_tiles.shape[0], panel_tiles.shape[2]), jnp.float32
    )
    for column_slot in range(panel_tiles.shape[1]):
        picked = jnp.take(left_panel, panel_columns[:, column_slot], axis=1)
        summed = summed + jnp.einsum(
            "rix,iyx->riy", picked, panel_tiles[:, column_slot], preferred_element_type=jnp.float32
        )
    return summed


def product_two(rounded, panel_tiles, panel_columns, panel_width):
    summed = jnp.zeros((rounded.shape[0], panel_width, panel_tiles.shape[3]), jnp.float32)
    for column_slot in range(panel_tiles.shape[1]):
        product = jnp.einsum(
            "rix,ixy->riy", rounded, panel_tiles[:, column_slot], preferred_element_type=jnp.float32
        )
        summed = summed.at[:, panel_columns[:, column_slot], :].add(product)
    return summed


def local(block_values, block_cols):
    tiles_here = block_values[0, :, 0]
    columns_here = block_cols[0, :, 0]
    tile_size = tiles_here.shape[2]
    slab_tiles = tiles_here.shape[0] * lax.axis_size("gx")
    left_tiles, left_columns = (
        picked_2(tiles_here[:WIN], "gy", 0),
        picked_2(columns_here[:WIN], "gy", 0),
    )
    left_panel = densify(left_tiles, left_columns, slab_tiles)
    height = left_panel.shape[0]
    on_diagonal = (lax.axis_index("gy") == lax.axis_index("gz")).astype(jnp.float32)
    panel_tiles, panel_columns = (
        lax.all_gather(tiles_here, "gx", axis=0, tiled=True),
        lax.all_gather(columns_here, "gx", axis=0, tiled=True),
    )
    partial_square = product_one(left_panel, panel_tiles, panel_columns)
    partial_square = partial_square.reshape(height, slab_tiles * tile_size)
    square = lax.psum(partial_square, "gz")
    square_low = square.astype(jnp.bfloat16).reshape(height, slab_tiles, tile_size)
    applied = product_two(square_low, panel_tiles, panel_columns, slab_tiles).reshape(
        height // lax.axis_size("gy") * lax.axis_size("gy"), slab_tiles * tile_size
    )
    return sent_and_summed(
        (3.0 * on_diagonal * square - 2.0 * applied).astype(jnp.bfloat16), "gy", 0
    )


def solution(mesh):
    in_specs = (P("gy", "gx", "gz", None, None, None), P("gy", "gx", "gz", None))
    out_specs = P(("gx", "gy"), "gz")
    return jax.shard_map(local, mesh=mesh, in_specs=in_specs, out_specs=out_specs, check_vma=False)
```

profile of v0, /device:TPU:32, one launch (start us, length us, event | category | flops | bytes accessed | tf_op | source)
XLA Modules:
  0.0 381.8 jit_solution(5912386459244780532)
XLA Ops:
  6.5 0.0 all-gather.6.cloned.1.call-start
  6.5 2.2 copy.30
  8.7 0.0 all-gather.6.cloned.1.call-update
  8.7 0.0 all-reduce.2.cloned.1.call-start
  8.8 9.7 %all-gather = s32[4,1,1,6]{3,2,1,0:T(1,128)S(1)} all-gather(s32[1,1,1,6]{3,2,1,0:T(1,128)S(1)} %slice-done.4), channel_id=2, replica_groups=mesh['gx'=16,'gy'=4,'gz'=4] {'gy'}, dimensions={0}, use_global_device_ids=true | all-gather | bytes 120 | tf_op jit(solution)/shard_map/all_gather | solution.py:10
  18.5 13.3 %all-gather.1 = bf16[4,1,1,6,128,128]{5,4,3,2,1,0:T(8,128)(2,1)S(1)} all-gather(bf16[1,1,1,6,128,128]{5,4,3,2,1,0:T(8,128)(2,1)S(1)} %slice-done.3), channel_id=3, replica_groups=mesh['gx'=16,'gy'=4,'gz'=4] {'gy'}, dimensions={0}, use_global_device_ids=true | all-gather | bytes 983040 | tf_op jit(solution)/shard_map/all_gather | solution.py:10
  31.8 0.8 convert_bitcast_fusion
  32.7 0.0 copy-start.5
  32.7 1.4 copy.29
  34.0 0.0 copy-done.5
  34.1 18.6 %all-gather.2 = s32[1,64,1,6]{3,2,0,1:T(1,128)S(1)} all-gather(s32[1,4,1,6]{3,2,0,1:T(1,128)S(1)} %bitcast.101), channel_id=4, replica_groups=mesh['gx'=16,'gy'=4,'gz'=4] {'gx'}, dimensions={1}, use_global_device_ids=true | all-gather | bytes 1632 | tf_op jit(solution)/shard_map/all_gather | solution.py:72
  52.7 0.4 fusion.41
  53.1 2.2 gather_fusion
  55.3 2.1 gather_fusion.4
  57.4 2.2 gather_fusion.3
  59.6 2.1 gather_fusion.2
  61.7 2.2 gather_fusion.1
  63.9 2.1 gather_fusion.5
  66.1 19.6 %all-gather.6.cloned.1.call-done = bf16[1,64,1,6,128,128]{5,4,1,3,2,0:T(8,128)(2,1)} async-done(((bf16[1,4,1,6,128,128]{5,4,1,3,2,0:T(8,128)(2,1)}), bf16[1,64,1,6,128,128]{5,4,1,3,2,0:T(8,128)(2,1)}) %all-gather.6.cloned.1.call-update) | async-done | bytes 12582928 | tf_op jit(solution)/shard_map/all_gather | solution.py:71
  85.7 6.2 %fusion.10 = f32[64,128,128]{1,2,0:T(8,128)} fusion(bf16[64,128,128]{2,1,0:T(8,128)(2,1)} %gather_fusion, pred[64]{0:T(512)(128)(4,1)S(1)} %get-tuple-element.29, bf16[64,6,128,128]{3,2,0,1:T(8,128)(2,1)} %bitcast.84), kind=kOutput, calls=%fused_computation.31 | convolution fusion | flops 269484032 | bytes 8388672 | tf_op jit(solution)/shard_map/rix,iyx->riy/dot_general | solution.py:42
  91.8 6.0 %fusion.2 = f32[64,128,128]{1,2,0:T(8,128)} fusion(bf16[64,128,128]{2,1,0:T(8,128)(2,1)} %gather_fusion.4, pred[64]{0:T(512)(128)(4,1)S(1)} %get-tuple-element.25, bf16[64,6,128,128]{3,2,0,1:T(8,128)(2,1)} %bitcast.85), kind=kOutput, calls=%fused_computation.23 | convolution fusion | flops 269484032 | bytes 8388672 | tf_op jit(solution)/shard_map/rix,iyx->riy/dot_general | solution.py:42
  97.8 3.6 fusion.4
  101.5 3.6 fusion.6
  105.1 3.6 fusion.8
  108.7 10.1 %add_add_fusion = f32[64,128,128]{1,2,0:T(8,128)} fusion(f32[64,128,128]{1,2,0:T(8,128)} %fusion.2, f32[64,128,128]{1,2,0:T(8,128)} %fusion.4, f32[64,128,128]{1,2,0:T(8,128)} %fusion.6, f32[64,128,128]{1,2,0:T(8,128)} %fusion.10, f32[64,128,128]{1,2,0:T(8,128)} %fusion.8, bf16[64,128,128]{2,1,0:T(8,128)(2,1)S(1)} %copy-done.4, ...), kind=kOutput, calls=%fused_computation.15 | convolution fusion | flops 274726912 | bytes 29360640 | tf_op jit(solution)/shard_map/rix,iyx->riy/dot_general | solution.py:42
  118.8 0.0 all-reduce.2.cloned.1.call-update
  118.8 98.5 %all-reduce.2.cloned.1.call-done = f32[128,8192]{0,1:T(8,128)} async-done(((f32[128,8192]{0,1:T(8,128)}), f32[128,8192]{0,1:T(8,128)}) %all-reduce.2.cloned.1.call-update) | async-done | bytes 4194320 | tf_op jit(solution)/shard_map/psum | solution.py:76
  217.4 2.5 convert_element_type.27
  219.9 0.0 slice-start.1
  219.9 4.6 %fusion.24 = f32[64,128,128]{2,1,0:T(8,128)} fusion(bf16[128,64,128]{0,2,1:T(8,128)(2,1)S(1)} %bitcast.78, bf16[64,6,128,128]{3,2,0,1:T(8,128)(2,1)} %bitcast.86), kind=kOutput, calls=%fused_computation.47 | convolution fusion | flops 268435456 | bytes 8388608 | tf_op jit(solution)/shard_map/rix,ixy->riy/dot_general | solution.py:51
  224.5 4.6 %fusion.25 = f32[64,128,128]{2,1,0:T(8,128)} fusion(bf16[128,64,128]{0,2,1:T(8,128)(2,1)S(1)} %bitcast.79, bf16[64,6,128,128]{3,2,0,1:T(8,128)(2,1)} %bitcast.87), kind=kOutput, calls=%fused_computation.48 | convolution fusion | flops 268435456 | bytes 8388608 | tf_op jit(solution)/shard_map/rix,ixy->riy/dot_general | solution.py:51
  229.1 2.8 fusion.26
  231.9 2.8 fusion.27
  234.7 2.8 fusion.28
  237.5 2.8 fusion.29
  240.3 2.5 broadcast_in_dim.11
  242.8 13.7 %scatter_fusion = f32[128,64,128]{2,0,1:T(8,128)} fusion(f32[128,64,128]{2,0,1:T(8,128)} %broadcast_in_dim.11, s32[64]{0:T(128)S(1)} %get-tuple-element.7, f32[64,128,128]{2,1,0:T(8,128)} %fusion.24), kind=kCustom, calls=%fused_computation.6 | custom fusion | flops 1048576 | bytes 12583168 | tf_op jit(solution)/shard_map/scatter-add | solution.py:54
  256.5 13.7 %scatter_fusion.1 = f32[128,64,128]{2,0,1:T(8,128)} fusion(f32[128,64,128]{2,0,1:T(8,128)} %scatter_fusion, s32[64]{0:T(128)S(1)} %get-tuple-element.8, f32[64,128,128]{2,1,0:T(8,128)} %fusion.25), kind=kCustom, calls=%fused_computation.7 | custom fusion | flops 1048576 | bytes 12583168 | tf_op jit(solution)/shard_map/scatter-add | solution.py:54
  270.2 13.7 %scatter_fusion.2 = f32[128,64,128]{2,0,1:T(8,128)} fusion(f32[128,64,128]{2,0,1:T(8,128)} %scatter_fusion.1, s32[64]{0:T(128)S(1)} %get-tuple-element.9, f32[64,128,128]{2,1,0:T(8,128)} %fusion.26), kind=kCustom, calls=%fused_computation.8 | custom fusion | flops 1048576 | bytes 12583168 | tf_op jit(solution)/shard_map/scatter-add | solution.py:54
  283.9 13.6 %scatter_fusion.3 = f32[128,64,128]{2,0,1:T(8,128)} fusion(f32[128,64,128]{2,0,1:T(8,128)} %scatter_fusion.2, s32[64]{0:T(128)S(1)} %get-tuple-element.10, f32[64,128,128]{2,1,0:T(8,128)} %fusion.27), kind=kCustom, calls=%fused_computation.9 | custom fusion | flops 1048576 | bytes 12583168 | tf_op jit(solution)/shard_map/scatter-add | solution.py:54
  297.5 13.7 %scatter_fusion.4 = f32[128,64,128]{2,0,1:T(8,128)} fusion(f32[128,64,128]{2,0,1:T(8,128)} %scatter_fusion.3, s32[64]{0:T(128)S(1)} %get-tuple-element.11, f32[64,128,128]{2,1,0:T(8,128)} %fusion.28), kind=kCustom, calls=%fused_computation.10 | custom fusion | flops 1048576 | bytes 12583168 | tf_op jit(solution)/shard_map/scatter-add | solution.py:54
  311.1 13.6 %scatter_fusion.5 = f32[128,64,128]{2,0,1:T(8,128)} fusion(f32[128,64,128]{2,0,1:T(8,128)} %scatter_fusion.4, s32[64]{0:T(128)S(1)} %get-tuple-element.6, f32[64,128,128]{2,1,0:T(8,128)} %fusion.29), kind=kCustom, calls=%fused_computation.11 | custom fusion | flops 1048576 | bytes 12583168 | tf_op jit(solution)/shard_map/scatter-add | solution.py:54
  324.8 4.7 %broadcast_multiply_fusion = f32[128,64,128]{2,0,1:T(8,128)} fusion(f32[128,64,128]{2,0,1:T(8,128)} %scatter_fusion.5), kind=kLoop, calls=%fused_computation.39 | loop fusion | flops 1048576 | bytes 8388608 | tf_op jit(solution)/shard_map/mul | solution.py:82
  329.5 5.6 %copy.42 = f32[128,64,128]{0,2,1:T(8,128)} copy(f32[128,64,128]{2,0,1:T(8,128)} %broadcast_multiply_fusion) | data formatting | bytes 8388608 | tf_op jit(solution)/shard_map/mul | solution.py:82
  335.1 5.2 %fusion = bf16[128,8192]{0,1:T(8,128)(2,1)} fusion(f32[128,64,128]{0,2,1:T(8,128)} %copy.42, f32[128,8192]{0,1:T(8,128)} %all-reduce.2.cloned.1.call-done, f32[]{:T(128)S(6)} %mul_shard_map.3), kind=kLoop, calls=%fused_computation.13 | loop fusion | flops 3145728 | bytes 10485764 | tf_op jit(solution)/shard_map/convert_element_type | solution.py:82
  340.3 2.9 copy.43
  343.3 30.4 %all_to_all.5 = bf16[4,32,8192]{2,1,0:T(8,128)(2,1)S(1)} all-to-all(bf16[4,32,8192]{2,1,0:T(8,128)(2,1)S(1)} %bitcast.99), channel_id=1, replica_groups=mesh['gx'=16,'gy'=4,'gz'=4] {'gy'}, dimensions={0} | all-to-all | bytes 4194304 | tf_op jit(solution)/shard_map/all_to_all | solution.py:21
  373.6 1.3 convert_reduce_fusion
  (34 shorter events, 0.1 us)
Async XLA Ops:
  6.5 12.0 %slice-start.3 = ((bf16[1,4,1,6,128,128]{5,4,3,2,1,0:T(8,128)(2,1)}), bf16[1,1,1,6,128,128]{5,4,3,2,1,0:T(8,128)(2,1)S(1)}, s32[]{:S(2)}) async-start(bf16[1,4,1,6,128,128]{5,4,3,2,1,0:T(8,128)(2,1)} %param.4), calls=%async_computation.6 | async-start | bytes 393216 | tf_op jit(solution)/shard_map/slice | solution.py:64
  6.5 2.2 slice-start.4
  6.5 79.1 %all-gather.6.cloned.1.call-start = ((), (), s32[]{:S(2)}) async-start(), calls=%async_computation.2 | async-start | bytes 13369344 | tf_op jit(solution)/shard_map/all_gather | solution.py:71
  8.7 208.6 %all-reduce.2.cloned.1.call-start = ((), (), s32[]{:S(2)}) async-start(), calls=%async_computation.1 | async-start | bytes 8388608 | tf_op jit(solution)/shard_map/psum | solution.py:76
  32.7 1.4 copy-start.5
  85.7 12.2 %copy-start = (bf16[1,64,1,6,128,128]{5,4,1,3,2,0:T(8,128)(2,1)S(1)}, bf16[1,64,1,6,128,128]{5,4,1,3,2,0:T(8,128)(2,1)}, u32[]{:S(2)}) copy-start(bf16[1,64,1,6,128,128]{5,4,1,3,2,0:T(8,128)(2,1)} %all-gather.6.cloned.1.call-done) | copy-start | bytes 37748740
  91.8 6.0 %copy-start.1 = (bf16[64,128,128]{2,1,0:T(8,128)(2,1)S(1)}, bf16[64,128,128]{2,1,0:T(8,128)(2,1)}, u32[]{:S(2)}) copy-start(bf16[64,128,128]{2,1,0:T(8,128)(2,1)} %gather_fusion.3) | copy-start | bytes 6291460
  97.8 3.6 copy-start.2
  101.5 3.6 copy-start.3
  105.1 3.6 copy-start.4
  217.4 11.7 %slice-start = ((s8[12582912]{0:T(1024)(128)(4,1)}), s8[4194304]{0:T(1024)(128)(4,1)S(1)}, s32[]{:S(2)}) async-start(s8[12582912]{0:T(1024)(128)(4,1)} %bitcast.92), calls=%async_computation.3 | async-start | bytes 8388608
  219.9 9.2 %slice-start.1 = ((s8[12582912]{0:T(1024)(128)(4,1)}), s8[4194304]{0:T(1024)(128)(4,1)S(1)}, s32[]{:S(2)}) async-start(s8[12582912]{0:T(1024)(128)(4,1)} %bitcast.92), calls=%async_computation.4 | async-start | bytes 8388608
  224.5 4.6 %slice-start.2 = ((s8[12582912]{0:T(1024)(128)(4,1)}), s8[4194304]{0:T(1024)(128)(4,1)S(1)}, s32[]{:S(2)}) async-start(s8[12582912]{0:T(1024)(128)(4,1)} %bitcast.92), calls=%async_computation.5 | async-start | bytes 8388608
Sparse Core Ops, SparseCore 0:
  9.2 76.4 all-gather.5
  118.9 98.3 all-reduce.1
where the time goes:
time: 383 us; the launch traced here: 382 us
  waiting for transfers between devices  118 us (31%)
  other arithmetic  96.3 us (25%)
  blocking collectives  72 us (19%)
  matrix products  54.3 us (14%)
  local copies, waits for them, and re-layouts  27.4 us (7%)
  between operations  13.5 us (4%)
    psum x1, waiting for transfers between devices, local(): square = lax.psum(partial_square, 'gz')  98.5 us
    scatter-add x6, other arithmetic, product_two(): summed = summed.at[:, panel_columns[:, column_slot], :].add(product)  82 us
    dot_general x6, matrix products, product_one(): jnp.einsum('rix,iyx->riy', picked, panel_tiles[:, column_slot], preferred...  33.1 us
    all_to_all x1, blocking collectives, sent_and_summed(): lax.all_to_all(tiles, axis, split_axis=0, concat_axis=0, tiled=True)  30.4 us
    all_gather x2, blocking collectives, picked_2(): lax.all_gather(x, axis)  23 us
    dot_general x6, matrix products, product_two(): jnp.einsum('rix,ixy->riy', rounded, panel_tiles[:, column_slot], preferre...  20.4 us
    all_gather x1, waiting for transfers between devices, local(): lax.all_gather(tiles_here, 'gx', axis=0, tiled=True)  19.6 us
    all_gather x1, blocking collectives, local(): lax.all_gather(columns_here, 'gx', axis=0, tiled=True)  18.6 us
  transfers between devices with their start and end apart: 2, of which 2 were waited for; matrix products, arithmetic and copies ran while one was open for 4% of the time, Pallas kernels for 0%

commit v1 on v0

--- a/solution.py
+++ b/solution.py
@@ -73,7 +73,9 @@
     )
     partial_square = product_one(left_panel, panel_tiles, panel_columns)
     partial_square = partial_square.reshape(height, slab_tiles * tile_size)
-    square = lax.psum(partial_square, "gz")
+    square = partial_square
+    for hop in (1, 2):
+        square = square + lax.ppermute(square, "gz", [(dev, dev ^ hop) for dev in range(4)])
     square_low = square.astype(jnp.bfloat16).reshape(height, slab_tiles, tile_size)
     applied = product_two(square_low, panel_tiles, panel_columns, slab_tiles).reshape(
         height // lax.axis_size("gy") * lax.axis_size("gy"), slab_tiles * tile_size

time: 383 us -> 480 us (1.25)
  waiting for transfers between devices: 118 us -> 200 us
  other arithmetic: 96.3 us -> 104 us
    ppermute x0 -> x2, waiting for transfers between devices: none -> 182 us  [local(): lax.ppermute(square, 'gz', [(dev, dev ^ hop) for dev in range(4)])]
    psum x1 -> x0, waiting for transfers between devices: 98.5 us -> none  [local(): square = lax.psum(partial_square, 'gz')]
  transfers between devices with their start and end apart: 2 -> 3, of which waited for: 2 -> 3; matrix products, arithmetic and copies ran while one was open for 4% -> 4% of each run, Pallas kernels for 0% -> 0%
where the time goes in v1:
time: 480 us; the launch traced here: 477 us
  waiting for transfers between devices  200 us (42%)
  other arithmetic  104 us (22%)
  blocking collectives  70.8 us (15%)
  matrix products  54.9 us (11%)
  local copies, waits for them, and re-layouts  29.1 us (6%)
  between operations  13.5 us (3%)
    ppermute x2, waiting for transfers between devices, local(): lax.ppermute(square, 'gz', [(dev, dev ^ hop) for dev in range(4)])  182 us
    scatter-add x6, other arithmetic, product_two(): summed = summed.at[:, panel_columns[:, column_slot], :].add(product)  82.2 us
    dot_general x6, matrix products, product_one(): jnp.einsum('rix,iyx->riy', picked, panel_tiles[:, column_slot], preferred...  33.1 us
    all_to_all x1, blocking collectives, sent_and_summed(): lax.all_to_all(tiles, axis, split_axis=0, concat_axis=0, tiled=True)  29.2 us
    all_gather x2, blocking collectives, picked_2(): lax.all_gather(x, axis)  23 us
    dot_general x6, matrix products, product_two(): jnp.einsum('rix,ixy->riy', rounded, panel_tiles[:, column_slot], preferre...  20.9 us
    all_gather x1, blocking collectives, local(): lax.all_gather(columns_here, 'gx', axis=0, tiled=True)  18.6 us
    all_gather x1, waiting for transfers between devices, local(): lax.all_gather(tiles_here, 'gx', axis=0, tiled=True)  18.1 us
  transfers between devices with their start and end apart: 3, of which 3 were waited for; matrix products, arithmetic and copies ran while one was open for 4% of the time, Pallas kernels for 0%

profile of v1, /device:TPU:32, one launch (start us, length us, event | category | flops | bytes accessed | tf_op | source)
XLA Modules:
  0.0 476.9 jit_solution(5308915799172064678)
XLA Ops:
  6.5 2.1 copy.30
  8.6 0.0 all-gather.6.cloned.1.call-update
  8.7 0.7 slice.58
  9.4 9.7 %all-gather = s32[4,1,1,6]{3,2,1,0:T(1,128)S(1)} all-gather(s32[1,1,1,6]{3,2,1,0:T(1,128)S(1)} %slice.58), channel_id=2, replica_groups=mesh['gx'=16,'gy'=4,'gz'=4] {'gy'}, dimensions={0}, use_global_device_ids=true | all-gather | bytes 120 | tf_op jit(solution)/shard_map/all_gather | solution.py:10
  19.1 0.9 slice.59
  20.0 13.3 %all-gather.1 = bf16[4,1,1,6,128,128]{5,4,3,2,1,0:T(8,128)(2,1)S(1)} all-gather(bf16[1,1,1,6,128,128]{5,4,3,2,1,0:T(8,128)(2,1)S(1)} %slice.59), channel_id=3, replica_groups=mesh['gx'=16,'gy'=4,'gz'=4] {'gy'}, dimensions={0}, use_global_device_ids=true | all-gather | bytes 983040 | tf_op jit(solution)/shard_map/all_gather | solution.py:10
  33.4 0.8 convert_bitcast_fusion
  34.2 1.4 copy.29
  35.6 18.6 %all-gather.2 = s32[1,64,1,6]{3,2,0,1:T(1,128)S(1)} all-gather(s32[1,4,1,6]{3,2,0,1:T(1,128)S(1)} %bitcast.102), channel_id=4, replica_groups=mesh['gx'=16,'gy'=4,'gz'=4] {'gx'}, dimensions={1}, use_global_device_ids=true | all-gather | bytes 1632 | tf_op jit(solution)/shard_map/all_gather | solution.py:72
  54.2 0.4 fusion.41
  54.6 2.2 gather_fusion
  56.8 2.1 gather_fusion.4
  58.9 2.2 gather_fusion.3
  61.1 2.1 gather_fusion.2
  63.2 2.2 gather_fusion.1
  65.4 2.1 gather_fusion.5
  67.6 18.1 %all-gather.6.cloned.1.call-done = bf16[1,64,1,6,128,128]{5,4,1,3,2,0:T(8,128)(2,1)} async-done(((bf16[1,4,1,6,128,128]{5,4,1,3,2,0:T(8,128)(2,1)}), bf16[1,64,1,6,128,128]{5,4,1,3,2,0:T(8,128)(2,1)}) %all-gather.6.cloned.1.call-update) | async-done | bytes 12582928 | tf_op jit(solution)/shard_map/all_gather | solution.py:71
  85.7 6.2 %fusion.10 = f32[64,128,128]{1,2,0:T(8,128)} fusion(bf16[64,128,128]{2,1,0:T(8,128)(2,1)} %gather_fusion, pred[64]{0:T(512)(128)(4,1)S(1)} %get-tuple-element.29, bf16[64,6,128,128]{3,2,0,1:T(8,128)(2,1)} %bitcast.85), kind=kOutput, calls=%fused_computation.31 | convolution fusion | flops 269484032 | bytes 8388672 | tf_op jit(solution)/shard_map/rix,iyx->riy/dot_general | solution.py:42
  91.8 6.0 %fusion.2 = f32[64,128,128]{1,2,0:T(8,128)} fusion(bf16[64,128,128]{2,1,0:T(8,128)(2,1)} %gather_fusion.4, pred[64]{0:T(512)(128)(4,1)S(1)} %get-tuple-element.25, bf16[64,6,128,128]{3,2,0,1:T(8,128)(2,1)} %bitcast.86), kind=kOutput, calls=%fused_computation.23 | convolution fusion | flops 269484032 | bytes 8388672 | tf_op jit(solution)/shard_map/rix,iyx->riy/dot_general | solution.py:42
  97.8 3.6 fusion.4
  101.5 3.6 fusion.6
  105.1 3.6 fusion.8
  108.7 10.1 %add_add_fusion = f32[64,128,128]{1,2,0:T(8,128)} fusion(f32[64,128,128]{1,2,0:T(8,128)} %fusion.2, f32[64,128,128]{1,2,0:T(8,128)} %fusion.4, f32[64,128,128]{1,2,0:T(8,128)} %fusion.6, f32[64,128,128]{1,2,0:T(8,128)} %fusion.10, f32[64,128,128]{1,2,0:T(8,128)} %fusion.8, bf16[64,128,128]{2,1,0:T(8,128)(2,1)S(1)} %copy-done.4, ...), kind=kOutput, calls=%fused_computation.15 | convolution fusion | flops 274726912 | bytes 29360640 | tf_op jit(solution)/shard_map/rix,iyx->riy/dot_general | solution.py:42
  118.8 1.5 collective-permute-start
  120.3 91.4 %collective-permute-done = f32[128,8192]{0,1:T(8,128)S(1)} collective-permute-done((f32[128,8192]{0,1:T(8,128)}, f32[128,8192]{0,1:T(8,128)S(1)}, u32[]{:S(2)}, u32[]{:S(2)}) %collective-permute-start) | collective-permute-done | bytes 4194336 | tf_op jit(solution)/shard_map/ppermute | solution.py:78
  211.7 4.7 bitcast_add_fusion
  216.4 3.0 collective-permute-start.1
  219.4 90.7 %collective-permute-done.1 = f32[128,8192]{0,1:T(8,128)} collective-permute-done((f32[128,8192]{0,1:T(8,128)}, f32[128,8192]{0,1:T(8,128)}, u32[]{:S(2)}, u32[]{:S(2)}) %collective-permute-start.1) | collective-permute-done | bytes 4194336 | tf_op jit(solution)/shard_map/ppermute | solution.py:78
  310.1 4.0 add_convert_fusion
  314.1 5.2 %fusion.24 = f32[64,128,128]{2,1,0:T(8,128)} fusion(bf16[128,64,128]{0,2,1:T(8,128)(2,1)S(1)} %bitcast.79, bf16[64,6,128,128]{3,2,0,1:T(8,128)(2,1)} %bitcast.87), kind=kOutput, calls=%fused_computation.47 | convolution fusion | flops 268435456 | bytes 8388608 | tf_op jit(solution)/shard_map/rix,ixy->riy/dot_general | solution.py:51
  319.3 4.4 fusion.25
  323.8 2.8 fusion.26
  326.6 2.8 fusion.27
  329.4 2.8 fusion.28
  332.3 2.8 fusion.29
  335.1 2.6 broadcast_in_dim.11
  337.6 13.9 %scatter_fusion = f32[128,64,128]{2,0,1:T(8,128)} fusion(f32[128,64,128]{2,0,1:T(8,128)} %broadcast_in_dim.11, s32[64]{0:T(128)S(1)} %get-tuple-element.7, f32[64,128,128]{2,1,0:T(8,128)} %fusion.24), kind=kCustom, calls=%fused_computation.6 | custom fusion | flops 1048576 | bytes 12583168 | tf_op jit(solution)/shard_map/scatter-add | solution.py:54
  351.5 13.7 %scatter_fusion.1 = f32[128,64,128]{2,0,1:T(8,128)} fusion(f32[128,64,128]{2,0,1:T(8,128)} %scatter_fusion, s32[64]{0:T(128)S(1)} %get-tuple-element.8, f32[64,128,128]{2,1,0:T(8,128)} %fusion.25), kind=kCustom, calls=%fused_computation.7 | custom fusion | flops 1048576 | bytes 12583168 | tf_op jit(solution)/shard_map/scatter-add | solution.py:54
  365.2 13.7 %scatter_fusion.2 = f32[128,64,128]{2,0,1:T(8,128)} fusion(f32[128,64,128]{2,0,1:T(8,128)} %scatter_fusion.1, s32[64]{0:T(128)S(1)} %get-tuple-element.9, f32[64,128,128]{2,1,0:T(8,128)} %fusion.26), kind=kCustom, calls=%fused_computation.8 | custom fusion | flops 1048576 | bytes 12583168 | tf_op jit(solution)/shard_map/scatter-add | solution.py:54
  378.9 13.7 %scatter_fusion.3 = f32[128,64,128]{2,0,1:T(8,128)} fusion(f32[128,64,128]{2,0,1:T(8,128)} %scatter_fusion.2, s32[64]{0:T(128)S(1)} %get-tuple-element.10, f32[64,128,128]{2,1,0:T(8,128)} %fusion.27), kind=kCustom, calls=%fused_computation.9 | custom fusion | flops 1048576 | bytes 12583168 | tf_op jit(solution)/shard_map/scatter-add | solution.py:54
  392.6 13.6 %scatter_fusion.4 = f32[128,64,128]{2,0,1:T(8,128)} fusion(f32[128,64,128]{2,0,1:T(8,128)} %scatter_fusion.3, s32[64]{0:T(128)S(1)} %get-tuple-element.11, f32[64,128,128]{2,1,0:T(8,128)} %fusion.28), kind=kCustom, calls=%fused_computation.10 | custom fusion | flops 1048576 | bytes 12583168 | tf_op jit(solution)/shard_map/scatter-add | solution.py:54
  406.2 13.7 %scatter_fusion.5 = f32[128,64,128]{2,0,1:T(8,128)} fusion(f32[128,64,128]{2,0,1:T(8,128)} %scatter_fusion.4, s32[64]{0:T(128)S(1)} %get-tuple-element.6, f32[64,128,128]{2,1,0:T(8,128)} %fusion.29), kind=kCustom, calls=%fused_computation.11 | custom fusion | flops 1048576 | bytes 12583168 | tf_op jit(solution)/shard_map/scatter-add | solution.py:54
  419.8 4.7 broadcast_multiply_fusion
  424.6 5.6 %copy.42 = f32[128,64,128]{0,2,1:T(8,128)} copy(f32[128,64,128]{2,0,1:T(8,128)} %broadcast_multiply_fusion) | data formatting | bytes 8388608 | tf_op jit(solution)/shard_map/mul | solution.py:84
  430.2 6.5 %fusion = bf16[128,8192]{0,1:T(8,128)(2,1)} fusion(f32[128,64,128]{0,2,1:T(8,128)} %copy.42, f32[]{:T(128)S(6)} %mul_shard_map.3, f32[128,8192]{0,1:T(8,128)} %bitcast_add_fusion, f32[128,8192]{0,1:T(8,128)} %collective-permute-done.1), kind=kLoop, calls=%fused_computation.13 | loop fusion | flops 4194304 | bytes 14680068 | tf_op jit(solution)/shard_map/convert_element_type | solution.py:84
  436.7 2.9 copy.43
  439.6 29.2 %all_to_all.5 = bf16[4,32,8192]{2,1,0:T(8,128)(2,1)S(1)} all-to-all(bf16[4,32,8192]{2,1,0:T(8,128)(2,1)S(1)} %bitcast.100), channel_id=1, replica_groups=mesh['gx'=16,'gy'=4,'gz'=4] {'gy'}, dimensions={0} | all-to-all | bytes 4194304 | tf_op jit(solution)/shard_map/all_to_all | solution.py:21
  468.8 1.3 convert_reduce_fusion
  (34 shorter events, 0.1 us)
Async XLA Ops:
  6.5 79.1 %all-gather.6.cloned.1.call-start = ((), (), s32[]{:S(2)}) async-start(), calls=%async_computation.1 | async-start | bytes 13369344 | tf_op jit(solution)/shard_map/all_gather | solution.py:71
  8.6 26.9 %copy-start.5 = (s32[1,4,1,6]{3,2,1,0:T(1,128)S(1)}, s32[1,4,1,6]{3,2,1,0:T(1,128)}, u32[]{:S(2)}) copy-start(s32[1,4,1,6]{3,2,1,0:T(1,128)} %param.5) | copy-start | bytes 292
  85.7 12.2 %copy-start = (bf16[1,64,1,6,128,128]{5,4,1,3,2,0:T(8,128)(2,1)S(1)}, bf16[1,64,1,6,128,128]{5,4,1,3,2,0:T(8,128)(2,1)}, u32[]{:S(2)}) copy-start(bf16[1,64,1,6,128,128]{5,4,1,3,2,0:T(8,128)(2,1)} %all-gather.6.cloned.1.call-done) | copy-start | bytes 37748740
  91.8 6.0 %copy-start.1 = (bf16[64,128,128]{2,1,0:T(8,128)(2,1)S(1)}, bf16[64,128,128]{2,1,0:T(8,128)(2,1)}, u32[]{:S(2)}) copy-start(bf16[64,128,128]{2,1,0:T(8,128)(2,1)} %gather_fusion.3) | copy-start | bytes 6291460
  97.8 3.6 copy-start.2
  101.5 3.6 copy-start.3
  105.1 3.6 copy-start.4
  118.8 92.9 %collective-permute-start = (f32[128,8192]{0,1:T(8,128)}, f32[128,8192]{0,1:T(8,128)S(1)}, u32[]{:S(2)}, u32[]{:S(2)}) collective-permute-start(f32[128,8192]{0,1:T(8,128)} %bitcast.99), channel_id=1, source_target_pairs={{0,1},{1,0},{2,3},{3,2},{4,5},{5,4},{6,7},{7,6},{8,9},{9,8},{10,11... | collective-permute-start | bytes 12582920 | tf_op jit(solution)/shard_map/ppermute | solution.py:78
  216.4 93.7 %collective-permute-start.1 = (f32[128,8192]{0,1:T(8,128)}, f32[128,8192]{0,1:T(8,128)}, u32[]{:S(2)}, u32[]{:S(2)}) collective-permute-start(f32[128,8192]{0,1:T(8,128)} %bitcast_add_fusion), channel_id=1, source_target_pairs={{0,2},{1,3},{2,0},{3,1},{4,6},{5,7},{6,4},{7,5},{8,10},{9,11},{10,... | collective-permute-start | bytes 12582920 | tf_op jit(solution)/shard_map/ppermute | solution.py:78
  310.1 13.7 %slice-start = ((s8[12582912]{0:T(1024)(128)(4,1)}), s8[4194304]{0:T(1024)(128)(4,1)S(1)}, s32[]{:S(2)}) async-start(s8[12582912]{0:T(1024)(128)(4,1)} %bitcast.93), calls=%async_computation.2 | async-start | bytes 8388608
  310.1 13.7 %slice-start.1 = ((s8[12582912]{0:T(1024)(128)(4,1)}), s8[4194304]{0:T(1024)(128)(4,1)S(1)}, s32[]{:S(2)}) async-start(s8[12582912]{0:T(1024)(128)(4,1)} %bitcast.93), calls=%async_computation.3 | async-start | bytes 8388608
  314.1 9.7 %slice-start.2 = ((s8[12582912]{0:T(1024)(128)(4,1)}), s8[4194304]{0:T(1024)(128)(4,1)S(1)}, s32[]{:S(2)}) async-start(s8[12582912]{0:T(1024)(128)(4,1)} %bitcast.93), calls=%async_computation.4 | async-start | bytes 8388608
Sparse Core Ops, SparseCore 0:
  9.2 76.4 all-gather.5
